TPU v7x, 128 devices: a whole 4x4x4 slice. The times are simulated.
128 devices in a mesh: row: 16 (over y, x_hi, core), col: 8 (over x_lo, z).
Axes of the slice: x: 4 (x_hi: 2, x_lo: 2; x = x_hi * 2 + x_lo), y: 4, z: 4, core: 2. Of those that a mesh axis runs over, the one named last changes fastest.
Arguments:
- matrix: float32 [8, 16, 128, 16, 8, 128], P(None, 'row', None, None, 'col'), may hold values from -6 to 6
- reflectors: float32 [16, 8, 128, 512], P(None, 'col'), as said below
Outputs:
- updated: float32 [8, 16, 128, 16, 8, 128], P(None, 'row', None, None, 'col')
Inputs may be any that keep to these rules, and one draw needn't show every extreme that they name: Read as a 16384 x 512 matrix, the columns of reflectors are orthonormal.
All inputs are finite; a program needn't handle non-finite values.
Results may differ from a plain program's by a relative error of at most 0.0001.
Values sent between devices are 32-bit elements; how exact they have to be, the bound alone decides.
A program may use at most 128 MiB of HBM per device.

v0:
```python
import jax
import jax.numpy as jnp
from jax import lax
from jax.sharding import PartitionSpec as P


def from_root(value, axis, source):
    kept = jnp.where(lax.axis_index(axis) == source, value, 0).astype(value.dtype)
    return lax.psum(kept, axis)


def rows_for(lines, peers):
    spare = -len(lines) % peers
    return jnp.pad(lines, [(0, spare)] + [(0, 0)] * (lines.ndim - 1))


def sum_by_parts(x, axis):
    lines = x.reshape(-1, *x.shape[1:][-1:])
    own = lax.psum_scatter(
        rows_for(lines, lax.axis_size(axis)), axis, scatter_dimension=0, tiled=True
    )
    whole = lax.all_gather(own, axis).reshape(-1, *lines.shape[1:])
    return lax.slice_in_dim(whole, 0, len(lines)).reshape(x.shape)


def per_device(matrix, reflectors):
    row_count = lax.axis_size("row")
    col_count = lax.axis_size("col")
    stride = row_count // col_count
    row_index = lax.axis_index("row")
    col_index = lax.axis_index("col")
    row_tiles, _, tile_size, col_tiles, _, _ = matrix.shape
    total_rank = reflectors.shape[3]
    local_rows = row_tiles * tile_size
    local_cols = col_tiles * tile_size
    current = matrix.reshape(local_rows, local_cols)
    row_ids = (
        (jnp.arange(row_tiles)[:, None] * row_count + row_index) * tile_size
        + jnp.arange(tile_size)[None, :]
    ).reshape(-1)
    col_ids = (
        (jnp.arange(col_tiles)[:, None] * col_count + col_index) * tile_size
        + jnp.arange(tile_size)[None, :]
    ).reshape(-1)
    lower_mask = row_ids[:, None] >= col_ids[None, :]
    strict_mask = row_ids[:, None] > col_ids[None, :]
    refl_cols = reflectors.reshape(local_cols, total_rank)

    def pick_rows(source):
        breadth = source.shape[1]
        blocks = source.reshape(row_tiles, stride, tile_size, breadth)
        chosen = lax.dynamic_index_in_dim(blocks, row_index // col_count, axis=1, keepdims=False)
        return chosen.reshape(local_rows, breadth)

    def matmul(left_side, right_side):
        return jnp.dot(
            left_side,
            right_side,
            precision=lax.Precision.HIGHEST,
            preferred_element_type=jnp.float32,
        )

    def inner(left_side, right_side):
        return lax.dot_general(
            left_side,
            right_side,
            (((0,), (0,)), ((), ())),
            precision=lax.Precision.HIGHEST,
            preferred_element_type=jnp.float32,
        )

    refl_rows = from_root(pick_rows(refl_cols), "col", row_index % col_count)
    direct_part = matmul(jnp.where(lower_mask, current, 0.0), refl_cols)
    trans_part = inner(jnp.where(strict_mask, current, 0.0), refl_rows)
    direct = lax.psum(direct_part, "col")
    transposed = sum_by_parts(trans_part, "row")
    w_rows = direct + from_root(pick_rows(transposed), "col", row_index % col_count)
    breadth = direct.shape[1]
    pieces = []
    for offset in range(stride):
        moved = from_root(direct, "row", col_index + offset * col_count)
        pieces.append(moved.reshape(row_tiles, tile_size, breadth))
    w_cols = transposed + jnp.stack(pieces, axis=1).reshape(local_cols, breadth)
    projection = lax.psum(inner(refl_rows, w_rows), "row")
    w_rows = w_rows - 0.5 * matmul(refl_rows, projection)
    w_cols = w_cols - 0.5 * matmul(refl_cols, projection)
    left_side = jnp.concatenate([refl_rows, w_rows], axis=1)
    right_side = jnp.concatenate([w_cols, refl_cols], axis=1)
    current = current - lax.dot_general(
        left_side,
        right_side,
        (((1,), (1,)), ((), ())),
        precision=lax.Precision.HIGHEST,
        preferred_element_type=jnp.float32,
    )
    return jnp.where(lower_mask, current, 0.0).reshape(matrix.shape)


def solution(mesh):
    placed = (P(None, "row", None, None, "col", None), P(None, "col", None, None))
    return jax.shard_map(
        per_device,
        mesh=mesh,
        in_specs=placed,
        out_specs=P(None, "row", None, None, "col", None),
        check_vma=False,
    )
```

profile of v0, /device:TPU:0, one launch (start us, length us, event | category | flops | bytes accessed | tf_op | source)
XLA Modules:
  0.0 595.8 jit_solution(9861063768099171922)
XLA Ops:
  6.5 3.2 bitcast_select_fusion.3
  9.8 0.0 all-reduce.6.cloned.1.call-update
  9.8 0.0 reduce-scatter.2.cloned.1.call-start
  9.9 0.1 iota_add_fusion.1
  9.9 0.1 iota_add_fusion
  10.0 84.9 %all-reduce.6.cloned.1.call-done = f32[1024,512]{1,0:T(8,128)} async-done(((f32[1024,512]{1,0:T(8,128)}), f32[1024,512]{1,0:T(8,128)}) %all-reduce.6.cloned.1.call-update) | async-done | bytes 2097168 | tf_op jit(solution)/shard_map/psum | solution.py:9
  94.9 19.6 %fusion.4 = f32[2048,512]{1,0:T(8,128)} fusion(f32[1024,512]{1,0:T(8,128)} %all-reduce.6.cloned.1.call-done, f32[128,8,16,128]{3,2,1,0:T(8,128)} %bitcast.60, s32[2048]{0:T(1024)S(1)} %get-tuple-element.16, s32[1024]{0:T(1024)S(1)} %get-tuple-element.14), kind=kOutput, calls=%fused_computation.7 | convolution fusion | flops 12889096192 | bytes 14692352 | tf_op jit(solution)/shard_map/dot_general | solution.py:64
  114.5 0.0 reduce-scatter.2.cloned.1.call-update
  114.5 0.0 all-gather.3.cloned.1.call-start
  114.5 80.9 %reduce-scatter.2.cloned.1.call-done = f32[128,512]{1,0:T(8,128)} async-done(((f32[2048,512]{1,0:T(8,128)}), f32[128,512]{1,0:T(8,128)}) %reduce-scatter.2.cloned.1.call-update) | async-done | bytes 262160 | tf_op jit(solution)/shard_map/reduce_scatter | solution.py:19
  195.4 0.0 all-gather.3.cloned.1.call-update
  195.5 0.2 all-reduce.10.cloned.1.call-start
  195.7 32.2 %fusion = f32[8,128,16,128]{3,2,1,0:T(8,128)} fusion(f32[8,1,128,16,1,128]{5,4,3,2,1,0:T(1,128)} %param.2, s32[16,128]{1,0:T(8,128)S(1)} %get-tuple-element.15, s32[8,128]{1,0:T(8,128)S(1)} %get-tuple-element.13), kind=kLoop, calls=%fused_computation.1 | loop fusion | flops 4194304 | bytes 16789504 | tf_op jit(solution)/shard_map/jit(_where)/select_n | solution.py:73
  227.9 20.0 %fusion.1 = f32[1024,512]{1,0:T(8,128)} fusion(f32[2048,512]{1,0:T(8,128)S(1)} %bitcast.54, f32[128,8,16,128]{3,2,1,0:T(8,128)} %bitcast.64), kind=kOutput, calls=%fused_computation.2 | convolution fusion | flops 12884901888 | bytes 14680064 | tf_op jit(solution)/shard_map/dot_general | solution.py:56
  247.9 3.5 all-gather.3.cloned.1.call-done
  251.5 3.2 bitcast_select_fusion.2
  254.7 0.0 all-reduce.10.cloned.1.call-update
  254.7 0.4 all-reduce.8.cloned.1.call-start
  255.2 103.2 %all-reduce.10.cloned.1.call-done = (f32[1024,512]{1,0:T(8,128)}, f32[1024,512]{1,0:T(8,128)}) async-done(((f32[1024,512]{1,0:T(8,128)}, f32[1024,512]{1,0:T(8,128)}), (f32[1024,512]{1,0:T(8,128)}, f32[1024,512]{1,0:T(8,128)})) %all-reduce.10.cloned.1.call-update) | async-done | bytes 4194320 | tf_op jit(solution)/shard_map/psum | solution.py:75
  358.4 5.4 fusion.27
  363.8 4.6 fusion.28
  368.4 0.0 all-reduce.8.cloned.1.call-update
  368.4 161.3 %all-reduce.8.cloned.1.call-done = (f32[8,1,128,512]{3,2,0,1:T(8,128)}, f32[8,1,128,512]{3,2,0,1:T(8,128)}, f32[512,512]{1,0:T(8,128)}) async-done(((f32[8,1,128,512]{3,2,0,1:T(8,128)}, f32[8,1,128,512]{3,2,0,1:T(8,128)}, f32[512,512]{1,0:T(8,128)}), (f32[8,1,128,512]{3,2,0,1:T(8,128)}, f32[8,1,128,512]{3,2,0,1:T(8,128)}, f32[512,512]{1,0:T(8,128)})) %all-reduce.8.cloned.1.call-update) | async-done | bytes 5242896 | tf_op jit(solution)/shard_map/psum | solution.py:9
  529.8 2.7 pad_maximum_fusion
  532.5 0.6 copy.5
  533.1 0.0 copy-start.1
  533.1 0.9 copy-done.4
  534.1 0.3 copy-done.5
  534.3 4.8 multiply_subtract_fusion
  539.1 7.5 %bitcast_subtract_fusion.1 = f32[2048,512]{1,0:T(8,128)S(1)} fusion(f32[2048,512]{1,0:T(8,128)S(1)} %copy-done.2, f32[8,2,128,512]{3,2,1,0:T(8,128)S(1)} %copy.5, f32[512,512]{1,0:T(8,128)S(1)} %copy-done.5, f32[2048,512]{1,0:T(8,128)S(1)} %bitcast.55), kind=kOutput, calls=%fused_computation.20 | convolution fusion | flops 6445596672 | bytes 17825792 | tf_op jit(solution)/shard_map/dot_general | solution.py:56
  546.7 33.6 %fusion.6 = f32[128,8,16,128]{3,1,2,0:T(8,128)} fusion(f32[128,8,16,128]{3,2,1,0:T(8,128)S(1)} %bitcast.63, s32[2048]{0:T(1024)S(1)} %get-tuple-element.16, s32[1024]{0:T(1024)S(1)} %get-tuple-element.14, f32[2048,512]{1,0:T(8,128)S(1)} %bitcast.56, f32[2048,512]{1,0:T(8,128)S(1)} %bitcast_subtract_fusion.1, f32[1024,512]{1,0:T(8,128)S(1)} %copy-done.6, ...), kind=kOutput, calls=%fused_computation.9 | convolution fusion | flops 25779240960 | bytes 29372416 | tf_op jit(solution)/shard_map/dot_general | solution.py:89
  580.3 8.8 %copy.11 = f32[128,8,16,128]{3,2,1,0:T(8,128)} copy(f32[128,8,16,128]{3,1,2,0:T(8,128)} %fusion.6) | data formatting | bytes 16777216
  (19 shorter events, 0.0 us)
Async XLA Ops:
  6.5 88.4 %all-reduce.6.cloned.1.call-start = ((), (), s32[]{:S(2)}) async-start(), calls=%async_computation.1 | async-start | bytes 4194304 | tf_op jit(solution)/shard_map/psum | solution.py:9
  9.8 185.7 %reduce-scatter.2.cloned.1.call-start = ((), (), s32[]{:S(2)}) async-start(), calls=%async_computation.2 | async-start | bytes 4456448 | tf_op jit(solution)/shard_map/reduce_scatter | solution.py:19
  114.5 137.0 %all-gather.3.cloned.1.call-start = ((), (), s32[]{:S(2)}) async-start(), calls=%async_computation.3 | async-start | bytes 4456448 | tf_op jit(solution)/shard_map/all_gather | solution.py:22
  195.5 162.9 %all-reduce.10.cloned.1.call-start = ((), (), s32[]{:S(2)}) async-start(), calls=%async_computation.5 | async-start | bytes 8388608 | tf_op jit(solution)/shard_map/psum | solution.py:75
  195.7 32.2 %copy-start = (f32[16,1,128,512]{3,2,1,0:T(8,128)S(1)}, f32[16,1,128,512]{3,2,1,0:T(8,128)}, u32[]{:S(2)}) copy-start(f32[16,1,128,512]{3,2,1,0:T(8,128)} %param.3) | copy-start | bytes 12582916
  254.7 275.0 %all-reduce.8.cloned.1.call-start = ((), (), s32[]{:S(2)}) async-start(), calls=%async_computation.4 | async-start | bytes 10485760 | tf_op jit(solution)/shard_map/psum | solution.py:9
  358.4 5.4 copy-start.3
  532.5 1.6 copy-start.4
  532.5 1.8 copy-start.5
  532.5 6.6 %copy-start.2 = (f32[2048,512]{1,0:T(8,128)S(1)}, f32[2048,512]{1,0:T(8,128)}, u32[]{:S(2)}) copy-start(f32[2048,512]{1,0:T(8,128)} %all-gather.3.cloned.1.call-done) | copy-start | bytes 12582916
  533.1 6.0 %copy-start.1 = (f32[16,1,128,512]{3,2,1,0:T(8,128)S(1)}, f32[16,1,128,512]{3,2,1,0:T(8,128)}, u32[]{:S(2)}) copy-start(f32[16,1,128,512]{3,2,1,0:T(8,128)} %param.3) | copy-start | bytes 12582916
  534.3 12.4 %slice-start = ((s8[8388608]{0:T(1024)(128)(4,1)}), s8[4194304]{0:T(1024)(128)(4,1)S(1)}, s32[]{:S(2)}) async-start(s8[8388608]{0:T(1024)(128)(4,1)} %bitcast.61), calls=%async_computation.6 | async-start | bytes 8388608
  539.1 7.6 %slice-start.1 = ((s8[8388608]{0:T(1024)(128)(4,1)}), s8[4194304]{0:T(1024)(128)(4,1)S(1)}, s32[]{:S(2)}) async-start(s8[8388608]{0:T(1024)(128)(4,1)} %bitcast.61), calls=%async_computation.7 | async-start | bytes 8388608
  539.1 7.6 %copy-start.6 = (f32[1024,512]{1,0:T(8,128)S(1)}, f32[1024,512]{1,0:T(8,128)}, u32[]{:S(2)}) copy-start(f32[1024,512]{1,0:T(8,128)} %multiply_subtract_fusion) | copy-start | bytes 6291460
Sparse Core Ops, SparseCore 0:
  9.9 84.9 all-reduce.5
  114.6 80.7 reduce-scatter.1
  197.9 53.5 all-gather.2
  254.8 103.4 all-reduce.9
  368.6 161.1 all-reduce.7
where the time goes:
time: 602 us; the launch traced here: 596 us
  waiting for transfers between devices  434 us (72%)
  matrix products  90.1 us (15%)
  other arithmetic  46.9 us (8%)
  between operations  13.5 us (2%)
  local copies, waits for them, and re-layouts  10.6 us (2%)
    psum x2, waiting for transfers between devices, from_root(): return lax.psum(kept, axis)  246 us
    psum x1, waiting for transfers between devices, per_device(): direct = lax.psum(direct_part, 'col')  103 us
    reduce_scatter x1, waiting for transfers between devices, sum_by_parts(): lax.psum_scatter(rows_for(lines, lax.axis_size(axis)), axis, scatter_dime...  80.9 us
    dot_general x1, matrix products, per_device(): lax.dot_general(left_side, right_side, (((1,), (1,)), ((), ())), precisio...  33.6 us
    dot_general x3, matrix products, matmul(): jnp.dot(left_side, right_side, precision=lax.Precision.HIGHEST, preferred...  32.4 us
    select_n x1, other arithmetic, per_device(): direct_part = matmul(jnp.where(lower_mask, current, 0.0), refl_cols)  32.2 us
    dot_general x2, matrix products, inner(): lax.dot_general(left_side, right_side, (((0,), (0,)), ((), ())), precisio...  24.2 us
  transfers between devices with their start and end apart: 5, of which 5 were waited for; matrix products, arithmetic and copies ran while one was open for 9% of the time, Pallas kernels for 0%

commit v1 on v0

--- a/solution.py
+++ b/solution.py
@@ -6,7 +6,7 @@
 
 def from_root(value, axis, source):
     kept = jnp.where(lax.axis_index(axis) == source, value, 0).astype(value.dtype)
-    return lax.psum(kept, axis)
+    return lax.all_gather(kept, axis).sum(axis=0)
 
 
 def rows_for(lines, peers):

time: 602 us -> 1210 us (2.01)
  waiting for transfers between devices: 434 us -> 986 us
  other arithmetic: 46.9 us -> 91.8 us
    all_gather x0 -> x4, waiting for transfers between devices: none -> 644 us  [from_root(): return lax.all_gather(kept, axis).sum(axis=0)]
    psum x2 -> x1, waiting for transfers between devices: 246 us -> 132 us  [per_device(): projection = lax.psum(inner(refl_rows, w_rows), 'row')]
    all_gather x1, waiting for transfers between devices: 3.54 us -> 56 us  [sum_by_parts(): whole = lax.all_gather(own, axis).reshape(-1, *lines.shape[1:])]
    reduce_sum x0 -> x4, other arithmetic: none -> 45.3 us  [from_root(): return lax.all_gather(kept, axis).sum(axis=0)]
    psum x1, waiting for transfers between devices: 103 us -> 74.1 us  [per_device(): direct = lax.psum(direct_part, 'col')]
  transfers between devices with their start and end apart: 5 -> 8, of which waited for: 5 -> 8; matrix products, arithmetic and copies ran while one was open for 9% -> 7% of each run, Pallas kernels for 0% -> 0%
where the time goes in v1:
time: 1210 us; the launch traced here: 1200 us
  waiting for transfers between devices  986 us (81%)
  other arithmetic  91.8 us (8%)
  matrix products  91.7 us (8%)
  between operations  14 us (1%)
    all_gather x4, waiting for transfers between devices, from_root(): return lax.all_gather(kept, axis).sum(axis=0)  644 us
    psum x1, waiting for transfers between devices, per_device(): projection = lax.psum(inner(refl_rows, w_rows), 'row')  132 us
    reduce_scatter x1, waiting for transfers between devices, sum_by_parts(): lax.psum_scatter(rows_for(lines, lax.axis_size(axis)), axis, scatter_dime...  79.4 us
    psum x1, waiting for transfers between devices, per_device(): direct = lax.psum(direct_part, 'col')  74.1 us
    all_gather x1, waiting for transfers between devices, sum_by_parts(): whole = lax.all_gather(own, axis).reshape(-1, *lines.shape[1:])  56 us
    reduce_sum x4, other arithmetic, from_root(): return lax.all_gather(kept, axis).sum(axis=0)  45.3 us
    dot_general x3, matrix products, matmul(): jnp.dot(left_side, right_side, precision=lax.Precision.HIGHEST, preferred...  33.7 us
    dot_general x1, matrix products, per_device(): lax.dot_general(left_side, right_side, (((1,), (1,)), ((), ())), precisio...  33.5 us
  transfers between devices with their start and end apart: 8, of which 8 were waited for; matrix products, arithmetic and copies ran while one was open for 7% of the time, Pallas kernels for 0%

profile of v1, /device:TPU:0, one launch (start us, length us, event | category | flops | bytes accessed | tf_op | source)
XLA Modules:
  0.0 1203.3 jit_solution(10605724246177749451)
XLA Ops:
  6.5 3.2 dynamic-slice_select_fusion.1
  9.8 0.0 reduce-scatter.2.cloned.1.call-start
  9.9 0.1 iota_add_fusion.1
  9.9 0.1 iota_add_fusion
  10.0 173.1 %all-gather.9.cloned.1.call-done = f32[8,1024,512]{2,1,0:T(8,128)} async-done(((f32[1,1024,512]{2,1,0:T(8,128)}), f32[8,1024,512]{2,1,0:T(8,128)}) %all-gather.9.cloned.1.call-update) | async-done | bytes 16777232 | tf_op jit(solution)/shard_map/all_gather | solution.py:9
  183.1 8.1 reduce_sum.36
  191.2 19.8 %fusion.4 = f32[2048,512]{1,0:T(8,128)} fusion(f32[1024,512]{1,0:T(8,128)S(1)} %reduce_sum.36, f32[128,8,16,128]{3,2,1,0:T(8,128)} %bitcast.60, s32[2048]{0:T(1024)S(1)} %get-tuple-element.11, s32[1024]{0:T(1024)S(1)} %get-tuple-element.9), kind=kOutput, calls=%fused_computation.7 | convolution fusion | flops 12889096192 | bytes 14692352 | tf_op jit(solution)/shard_map/dot_general | solution.py:64
  211.1 79.4 %reduce-scatter.2.cloned.1.call-done = f32[128,512]{1,0:T(8,128)} async-done(((f32[2048,512]{1,0:T(8,128)}), f32[128,512]{1,0:T(8,128)}) %reduce-scatter.2.cloned.1.call-update) | async-done | bytes 262160 | tf_op jit(solution)/shard_map/reduce_scatter | solution.py:19
  290.6 56.0 %all-gather.13.cloned.1.call-done = f32[2048,512]{1,0:T(8,128)} async-done(((f32[128,512]{1,0:T(8,128)}), f32[2048,512]{1,0:T(8,128)}) %all-gather.13.cloned.1.call-update) | async-done | bytes 4194320 | tf_op jit(solution)/shard_map/all_gather | solution.py:22
  346.6 3.2 dynamic-slice_select_fusion
  349.8 0.3 all-reduce.3.cloned.1.call-start
  350.1 32.2 %fusion = f32[8,128,16,128]{3,2,1,0:T(8,128)} fusion(f32[8,1,128,16,1,128]{5,4,3,2,1,0:T(1,128)} %param.2, s32[16,128]{1,0:T(8,128)S(1)} %get-tuple-element.10, s32[8,128]{1,0:T(8,128)S(1)} %get-tuple-element.8), kind=kLoop, calls=%fused_computation.1 | loop fusion | flops 4194304 | bytes 16789504 | tf_op jit(solution)/shard_map/jit(_where)/select_n | solution.py:73
  382.3 19.5 %fusion.1 = f32[1024,512]{1,0:T(8,128)} fusion(f32[2048,512]{1,0:T(8,128)S(1)} %bitcast.54, f32[128,8,16,128]{3,2,1,0:T(8,128)} %bitcast.64), kind=kOutput, calls=%fused_computation.2 | convolution fusion | flops 12884901888 | bytes 14680064 | tf_op jit(solution)/shard_map/dot_general | solution.py:56
  401.9 116.7 %all-gather.11.cloned.1.call-done = f32[8,1024,512]{2,1,0:T(8,128)} async-done(((f32[1,1024,512]{2,1,0:T(8,128)}), f32[8,1024,512]{2,1,0:T(8,128)}) %all-gather.11.cloned.1.call-update) | async-done | bytes 16777232 | tf_op jit(solution)/shard_map/all_gather | solution.py:9
  518.6 9.4 reduce_sum.37
  528.0 74.1 %all-reduce.3.cloned.1.call-done = f32[1024,512]{1,0:T(8,128)} async-done(((f32[1024,512]{1,0:T(8,128)}), f32[1024,512]{1,0:T(8,128)}) %all-reduce.3.cloned.1.call-update) | async-done | bytes 2097168 | tf_op jit(solution)/shard_map/psum | solution.py:75
  602.1 5.4 fusion.27
  607.5 4.7 fusion.28
  612.3 0.7 all-gather.17.cloned.1.call-update
  613.0 8.8 all-gather.15.cloned.1.call-start
  621.8 132.1 %all-reduce.5.cloned.1.call-done = f32[512,512]{1,0:T(8,128)} async-done(((f32[512,512]{1,0:T(8,128)}), f32[512,512]{1,0:T(8,128)}) %all-reduce.5.cloned.1.call-update) | async-done | bytes 1048592 | tf_op jit(solution)/shard_map/psum | solution.py:84
  753.8 6.7 multiply_subtract_fusion
  760.5 182.1 %all-gather.17.cloned.1.call-done = f32[16384,512]{1,0:T(8,128)} async-done(((f32[1024,512]{1,0:T(8,128)}), f32[16384,512]{1,0:T(8,128)}) %all-gather.17.cloned.1.call-update) | async-done | bytes 33554448 | tf_op jit(solution)/shard_map/all_gather | solution.py:9
  942.6 13.8 %reduce_sum.39 = f32[1024,512]{1,0:T(8,128)S(1)} reduce(f32[16,1024,512]{2,1,0:T(8,128)} %bitcast.51, f32[]{:T(128)} %constant.57.clone.1), dimensions={0}, to_apply=%region_6.7 | reduce | flops 7864320 | bytes 35651588 | tf_op jit(solution)/shard_map/reduce_sum | solution.py:9
  956.4 171.7 %all-gather.15.cloned.1.call-done = f32[16384,512]{1,0:T(8,128)} async-done(((f32[1024,512]{1,0:T(8,128)}), f32[16384,512]{1,0:T(8,128)}) %all-gather.15.cloned.1.call-update) | async-done | bytes 33554448 | tf_op jit(solution)/shard_map/all_gather | solution.py:9
  1128.0 14.1 %reduce_sum.38 = f32[1024,512]{1,0:T(8,128)} reduce(f32[16,1024,512]{2,1,0:T(8,128)} %bitcast.52, f32[]{:T(128)} %constant.57.clone.1), dimensions={0}, to_apply=%region_5.6 | reduce | flops 7864320 | bytes 35651588 | tf_op jit(solution)/shard_map/reduce_sum | solution.py:9
  1142.1 2.2 pad_maximum_fusion
  1144.4 0.6 copy-done.4
  1145.0 1.3 copy-done.5
  1146.2 7.5 bitcast_subtract_fusion.1
  1153.8 33.5 %fusion.6 = f32[128,8,16,128]{3,1,2,0:T(8,128)} fusion(f32[128,8,16,128]{3,2,1,0:T(8,128)S(1)} %bitcast.63, s32[2048]{0:T(1024)S(1)} %get-tuple-element.11, s32[1024]{0:T(1024)S(1)} %get-tuple-element.9, f32[2048,512]{1,0:T(8,128)S(1)} %bitcast.56, f32[2048,512]{1,0:T(8,128)S(1)} %bitcast_subtract_fusion.1, f32[1024,512]{1,0:T(8,128)S(1)} %copy-done.7, ...), kind=kOutput, calls=%fused_computation.9 | convolution fusion | flops 25779240960 | bytes 29372416 | tf_op jit(solution)/shard_map/dot_general | solution.py:89
  1187.3 8.8 copy.7
  (33 shorter events, 0.3 us)
Async XLA Ops:
  6.5 176.6 %all-gather.9.cloned.1.call-start = ((), (), s32[]{:S(2)}) async-start(), calls=%async_computation.1 | async-start | bytes 18874368 | tf_op jit(solution)/shard_map/all_gather | solution.py:9
  9.8 280.7 %reduce-scatter.2.cloned.1.call-start = ((), (), s32[]{:S(2)}) async-start(), calls=%async_computation.3 | async-start | bytes 4456448 | tf_op jit(solution)/shard_map/reduce_scatter | solution.py:19
  191.2 19.8 %copy-start = (f32[1024,512]{1,0:T(8,128)}, f32[1024,512]{1,0:T(8,128)S(1)}, u32[]{:S(2)}) copy-start(f32[1024,512]{1,0:T(8,128)S(1)} %reduce_sum.36) | copy-start | bytes 6291460
  211.0 135.5 %all-gather.13.cloned.1.call-start = ((), (), s32[]{:S(2)}) async-start(), calls=%async_computation.6 | async-start | bytes 4456448 | tf_op jit(solution)/shard_map/all_gather | solution.py:22
  290.5 228.0 %all-gather.11.cloned.1.call-start = ((), (), s32[]{:S(2)}) async-start(), calls=%async_computation.4 | async-start | bytes 18874368 | tf_op jit(solution)/shard_map/all_gather | solution.py:9
  349.8 252.3 %all-reduce.3.cloned.1.call-start = ((), (), s32[]{:S(2)}) async-start(), calls=%async_computation.2 | async-start | bytes 4194304 | tf_op jit(solution)/shard_map/psum | solution.py:75
  350.1 32.2 %copy-start.3 = (f32[16,1,128,512]{3,2,1,0:T(8,128)S(1)}, f32[16,1,128,512]{3,2,1,0:T(8,128)}, u32[]{:S(2)}) copy-start(f32[16,1,128,512]{3,2,1,0:T(8,128)} %param.3) | copy-start | bytes 12582916
  401.9 352.0 %all-reduce.5.cloned.1.call-start = ((), (), s32[]{:S(2)}) async-start(), calls=%async_computation.5 | async-start | bytes 2097152 | tf_op jit(solution)/shard_map/psum | solution.py:84
  602.1 5.4 copy-start.1
  612.2 330.4 %all-gather.17.cloned.1.call-start = ((), (), s32[]{:S(2)}) async-start(), calls=%async_computation.8 | async-start | bytes 35651584 | tf_op jit(solution)/shard_map/all_gather | solution.py:9
  613.0 515.1 %all-gather.15.cloned.1.call-start = ((), (), s32[]{:S(2)}) async-start(), calls=%async_computation.7 | async-start | bytes 35651584 | tf_op jit(solution)/shard_map/all_gather | solution.py:9
  1128.0 16.3 %copy-start.6 = (f32[512,512]{1,0:T(8,128)S(1)}, f32[512,512]{1,0:T(8,128)}, u32[]{:S(2)}) copy-start(f32[512,512]{1,0:T(8,128)} %all-reduce.5.cloned.1.call-done) | copy-start | bytes 3145732
  1142.1 2.8 copy-start.4
  1142.1 4.1 copy-start.5
  1142.1 11.6 slice-start
  1146.2 7.6 copy-start.2
  1146.2 7.6 slice-start.1
  1146.2 7.6 copy-start.7
Sparse Core Ops, SparseCore 0:
  9.9 173.1 all-gather.8
  211.2 79.3 reduce-scatter.1
  293.0 53.5 all-gather.12
  349.9 168.5 all-gather.10
  520.9 81.0 all-reduce.2
  612.3 141.4 all-reduce.4
  756.3 186.2 all-gather.16
  945.1 182.9 all-gather.14
